TPU v7x, 32 devices: a whole 2x2x4 slice. The times are simulated.
32 devices in a mesh: rep: 4 (over x, core), shard: 8 (over z, y).
Axes of the slice: x: 2, y: 2, z: 4, core: 2. Of those that a mesh axis runs over, the one named last changes fastest.
Arguments:
- dense_out: bfloat16 [4096, 128], P(('rep', 'shard')), may hold values from -0.75 to 0.75
- pooled: bfloat16 [4096, 26, 128], P(('rep', 'shard')), may hold values from -0.75 to 0.75
- top_weight: bfloat16 [479, 1024], replicated, may hold values from -0.25 to 0.25
- top_cotangent: bfloat16 [4096, 1024], P(('rep', 'shard')), may hold values from -3 to 3
- indices: int32 [4096, 26, 2], P(('rep', 'shard')), may hold values from 0 to 2047, as said below
Outputs:
- dense_grad: bfloat16 [4096, 128], P(('rep', 'shard'))
- top_grad: float32 [479, 1024], replicated
- bias_grad: float32 [1024], replicated
- table_grad: float32 [26, 2048, 128], P(None, 'shard')
Inputs may be any that keep to these rules, and one draw needn't show every extreme that they name: `indices`: rows r with r // 256 = s are held by shard s. For every device's 128 samples and every table, at most 16 of the device's lookups fall in any one block of 64 rows starting at a multiple of 64, and some such block holds exactly 16.
All inputs are finite; a program needn't handle non-finite values.
Results may differ from a plain program's by a relative error of at most 0.008.
Values may be sent and summed in bfloat16 or wider, within the bound.
A program may use at most 128 MiB of HBM per device.

v0:
```python
import jax
import jax.numpy as jnp
import numpy as np
from jax import lax
from jax.sharding import PartitionSpec as P

R_SHARD = 256
highest = lax.Precision.HIGHEST


def one_hot_sums(rows, keys, height):
    tables_here = rows.shape[0]
    flat_rows = rows.reshape(tables_here, -1, rows.shape[-1])
    flat_keys = keys.reshape(tables_here, -1)

    def per_table(member):
        table_rows, table_keys = member
        levels = lax.broadcasted_iota(jnp.int32, (height, table_keys.shape[0]), 0)
        matches = (levels == table_keys[None, :]).astype(jnp.bfloat16)
        return jnp.dot(matches, table_rows, preferred_element_type=jnp.float32)

    return lax.map(per_table, (flat_rows, flat_keys))


def pair_table(vectors):
    lower_i, lower_j = np.tril_indices(vectors, -1)
    select = np.zeros((vectors * vectors, lower_i.shape[0]), np.float32)
    select[lower_i * vectors + lower_j, np.arange(lower_i.shape[0])] = 1.0
    mirrored = np.zeros((lower_i.shape[0], vectors * vectors), np.float32)
    mirrored[np.arange(lower_i.shape[0]), lower_i * vectors + lower_j] = 1.0
    mirrored[np.arange(lower_i.shape[0]), lower_j * vectors + lower_i] = 1.0
    return (jnp.asarray(select), jnp.asarray(mirrored))


def on_device(dense_out, pooled, top_weight, top_cotangent, indices):
    samples = dense_out.shape[0]
    emb_width = dense_out.shape[1]
    tables = pooled.shape[1]
    lookups = indices.shape[2]
    replicas = lax.axis_size("rep")
    shards = lax.axis_size("shard")
    vectors = tables + 1
    select, mirrored = pair_table(vectors)
    stacked = jnp.concatenate([dense_out[:, None, :], pooled], axis=1)
    gram_matrix = jnp.einsum("bie,bje->bij", stacked, stacked, preferred_element_type=jnp.float32)
    gram_flat = gram_matrix.reshape(samples, vectors * vectors)
    pair_values = jnp.dot(
        gram_flat, select, precision=highest, preferred_element_type=jnp.float32
    ).astype(jnp.bfloat16)
    joined = jnp.concatenate([dense_out, pair_values], axis=1)
    grad_in = lax.dot_general(
        top_cotangent, top_weight, (((1,), (1,)), ((), ())), preferred_element_type=jnp.float32
    )
    top_part = lax.dot_general(
        joined, top_cotangent, (((0,), (0,)), ((), ())), preferred_element_type=jnp.float32
    )
    bias_part = jnp.sum(top_cotangent, axis=0, dtype=jnp.float32)
    pair_grad = grad_in[:, emb_width:]
    mirror = jnp.dot(
        pair_grad, mirrored, precision=highest, preferred_element_type=jnp.float32
    ).reshape(samples, vectors, vectors)
    mirror_high = mirror.astype(jnp.bfloat16)
    mirror_low = (mirror - mirror_high.astype(jnp.float32)).astype(jnp.bfloat16)
    vec_grad = jnp.einsum("bij,bje->bie", mirror_high, stacked, preferred_element_type=jnp.float32)
    vec_grad = vec_grad + jnp.einsum(
        "bij,bje->bie", mirror_low, stacked, preferred_element_type=jnp.float32
    )
    dense_grad = (grad_in[:, :emb_width] + vec_grad[:, 0]).astype(jnp.bfloat16)
    pooled_grad = vec_grad[:, 1:].astype(jnp.bfloat16)
    row_span = R_SHARD // replicas
    blocks = replicas * shards
    per_block = 2 * samples * lookups // blocks
    count_here = samples * lookups
    capacity = blocks * per_block
    by_table = jnp.transpose(indices, (1, 0, 2)).reshape(tables, count_here)
    lookup_rows = jnp.broadcast_to(
        jnp.transpose(pooled_grad, (1, 0, 2))[:, :, None, :], (tables, samples, lookups, emb_width)
    ).reshape(tables, count_here, emb_width)

    def place_table(member):
        table_keys, table_rows = member
        block_row = table_keys // row_span
        later = lax.broadcasted_iota(jnp.int32, (count_here, count_here), 0)
        sooner = lax.broadcasted_iota(jnp.int32, (count_here, count_here), 1)
        earlier = (block_row[None, :] == block_row[:, None]) & (sooner < later)
        slot_row = block_row * per_block + jnp.sum(earlier, axis=1, dtype=jnp.int32)
        levels = lax.broadcasted_iota(jnp.int32, (capacity, count_here), 0)
        placed = levels == slot_row[None, :]
        rows_out = jnp.dot(
            placed.astype(jnp.bfloat16), table_rows, preferred_element_type=jnp.float32
        ).astype(jnp.bfloat16)
        keys_out = (
            jnp.sum(
                jnp.where(placed, (table_keys % R_SHARD + 1)[None, :], 0), axis=1, dtype=jnp.int32
            )
            - 1
        )
        return (rows_out, keys_out)

    send_rows, send_keys = lax.map(place_table, (by_table, lookup_rows))
    top_grad, bias_grad = lax.psum((top_part, bias_part), ("rep", "shard"))
    grouped_rows = send_rows.reshape(tables, shards, replicas * per_block, emb_width)
    grouped_keys = send_keys.reshape(tables, shards, replicas * per_block)
    partial_value = one_hot_sums(
        lax.all_to_all(grouped_rows, "shard", split_axis=1, concat_axis=1, tiled=True),
        lax.all_to_all(grouped_keys, "shard", split_axis=1, concat_axis=1, tiled=True),
        R_SHARD,
    )
    table_grad = lax.psum(partial_value, "rep")
    return (dense_grad, top_grad, bias_grad, table_grad)


def solution(mesh):
    return jax.shard_map(
        on_device,
        mesh=mesh,
        in_specs=(
            P(("rep", "shard"), None),
            P(("rep", "shard"), None, None),
            P(),
            P(("rep", "shard"), None),
            P(("rep", "shard"), None, None),
        ),
        out_specs=(P(("rep", "shard"), None), P(), P(), P(None, "shard", None)),
        check_vma=False,
    )
```

profile of v0, /device:TPU:0, one launch (start us, length us, event | category | flops | bytes accessed | tf_op | source)
XLA Modules:
  0.0 386.4 jit_solution(17738884548787175198)
XLA Ops:
  9.8 2.0 fusion.17
  17.7 2.8 copy.78
  20.6 2.4 copy.77
  23.0 1.8 fusion.15
  24.8 2.9 copy.79
  27.7 2.2 add.78
  34.0 2.4 broadcast_in_dim.67
  36.3 57.8 %while.25 = (s32[]{:T(128)}, bf16[26,512,128]{2,1,0:T(8,128)(2,1)}, s32[26,512]{1,0:T(8,128)S(1)}, s32[26,256]{1,0:T(8,128)S(1)}, bf16[26,256,128]{2,1,0:T(8,128)(2,1)}, /*index=5*/s32[]{:T(128)}, s32[]{:T(128)}) while((s32[]{:T(128)}, bf16[26,512,128]{2,1,0:T(8,128)(2,1)}, s32[26,512]{1,0:T(8,128)S(1)}, s32[26,256]{1,0:T(8,128)S(1)}, ...), condition=%wide.region_6.7_spmd, body=%wide.region_3.6_spmd.sunk | while | flops 34486784 | bytes 224341 | solution.py:100
  95.0 7.3 %all-to-all-start = ((s32[8,1,1664]{2,1,0:T(1,128)}), s32[8,1,1664]{2,1,0:T(1,128)S(1)}, u32[]{:S(2)}, u32[]{:S(2)}) async-start(s32[8,1,1664]{2,1,0:T(1,128)} %reshape.98), calls=%async_computation | async-start | bytes 106496 | tf_op jit(solution)/shard_map/all_to_all | solution.py:106
  102.3 4.8 %copy.87 = bf16[26,8,64,128]{3,2,0,1:T(8,128)(2,1)} copy(bf16[26,8,64,128]{3,2,1,0:T(8,128)(2,1)} %bitcast.71) | data formatting | bytes 6815744 | tf_op jit(solution)/shard_map/reshape | solution.py:102
  107.1 2.0 all-to-all-done
  109.1 4.5 %all-to-all-start.1 = ((bf16[26,8,64,128]{3,2,0,1:T(8,128)(2,1)}), bf16[26,8,64,128]{3,2,0,1:T(8,128)(2,1)}, u32[]{:S(2)}, u32[]{:S(2)}) async-start(bf16[26,8,64,128]{3,2,0,1:T(8,128)(2,1)} %copy.87), calls=%async_computation.1 | async-start | bytes 6815744 | tf_op jit(solution)/shard_map/all_to_all | solution.py:105
  114.5 2.0 fusion.14
  116.5 2.9 reshape.97
  119.4 2.0 convolution_convert_fusion.1
  124.8 73.4 %all-to-all-done.1 = bf16[26,8,64,128]{3,2,0,1:T(8,128)(2,1)} async-done(((bf16[26,8,64,128]{3,2,0,1:T(8,128)(2,1)}), bf16[26,8,64,128]{3,2,0,1:T(8,128)(2,1)}, u32[]{:S(2)}, u32[]{:S(2)}) %all-to-all-start.1) | async-done | bytes 3407904 | tf_op jit(solution)/shard_map/all_to_all | solution.py:105
  198.2 4.8 %copy.88 = bf16[26,8,64,128]{3,2,1,0:T(8,128)(2,1)} copy(bf16[26,8,64,128]{3,2,0,1:T(8,128)(2,1)} %all-to-all-done.1) | data formatting | bytes 6815744 | tf_op jit(solution)/shard_map/all_to_all | solution.py:105
  203.0 47.0 %while.26 = (s32[]{:T(128)}, f32[26,256,128]{2,1,0:T(8,128)}, s32[26,512]{1,0:T(8,128)S(1)}, bf16[26,512,128]{2,1,0:T(8,128)(2,1)}, s32[]{:T(128)}) while((s32[]{:T(128)}, f32[26,256,128]{2,1,0:T(8,128)}, s32[26,512]{1,0:T(8,128)S(1)}, bf16[26,512,128]{2,1,0:T(8,128)(2,1)}, s32[]{:T(128)}) %tuple.72), condition=%wide.region_8.9_spmd, body=%wide.region_7.8_spmd.sunk | while | flops 33685504 | bytes 269377 | solution.py:22
  203.0 1.8 fusion.47
  204.8 1.8 fusion.47
  206.6 1.8 fusion.47
  208.4 1.8 fusion.47
  210.2 1.8 fusion.47
  212.0 1.8 fusion.47
  213.9 1.8 fusion.47
  215.7 1.8 fusion.47
  217.5 1.8 fusion.47
  219.3 1.8 fusion.47
  221.1 1.8 fusion.47
  222.9 1.8 fusion.47
  224.7 1.8 fusion.47
  226.5 1.8 fusion.47
  228.3 1.8 fusion.47
  230.1 1.8 fusion.47
  231.9 1.8 fusion.47
  233.7 1.8 fusion.47
  235.5 1.8 fusion.47
  237.3 1.8 fusion.47
  239.2 1.8 fusion.47
  241.0 1.8 fusion.47
  242.8 1.8 fusion.47
  244.6 1.8 fusion.47
  246.4 1.8 fusion.47
  248.2 1.8 fusion.47
  251.6 38.0 %psum.22 = f32[1024]{0:T(1024)} all-reduce(f32[1024]{0:T(1024)S(1)} %convert_reduce_fusion.1), channel_id=1, replica_groups=mesh['rep'=4,'shard'=8] {'rep','shard'}, use_global_device_ids=true, to_apply=%region_2.3 | all-reduce | flops 1024 | bytes 8192 | tf_op jit(solution)/shard_map/psum | solution.py:101
  289.6 10.4 %all-reduce.3.cloned.1.call-done = f32[479,1024]{1,0:T(8,128)} async-done(((f32[479,1024]{1,0:T(8,128)}), f32[479,1024]{1,0:T(8,128)}) %all-reduce.3.cloned.1.call-update) | async-done | bytes 1962000 | tf_op jit(solution)/shard_map/psum | solution.py:101
  300.1 74.5 %all-reduce.5.cloned.1.call-done = f32[26,256,128]{2,1,0:T(8,128)} async-done(((f32[26,256,128]{2,1,0:T(8,128)}), f32[26,256,128]{2,1,0:T(8,128)}) %all-reduce.5.cloned.1.call-update) | async-done | bytes 3407888 | tf_op jit(solution)/shard_map/psum | solution.py:109
  374.6 3.2 copy.115
  (310 shorter events, 78.0 us)
Async XLA Ops:
  7.2 1.2 copy-start
  7.2 2.6 copy-start.5
  11.8 4.1 %copy-start.7 = (bf16[128,128]{1,0:T(8,128)(2,1)S(1)}, bf16[128,128]{1,0:T(8,128)(2,1)}, u32[]{:S(2)}) copy-start(bf16[128,128]{1,0:T(8,128)(2,1)} %param.11) | copy-start | bytes 98308
  29.9 1.3 copy-start.1
  31.1 2.6 copy-start.8
  95.0 14.1 %all-to-all-start = ((s32[8,1,1664]{2,1,0:T(1,128)}), s32[8,1,1664]{2,1,0:T(1,128)S(1)}, u32[]{:S(2)}, u32[]{:S(2)}) async-start(s32[8,1,1664]{2,1,0:T(1,128)} %reshape.98), calls=%async_computation | async-start | bytes 106496 | tf_op jit(solution)/shard_map/all_to_all | solution.py:106
  109.1 89.1 %all-to-all-start.1 = ((bf16[26,8,64,128]{3,2,0,1:T(8,128)(2,1)}), bf16[26,8,64,128]{3,2,0,1:T(8,128)(2,1)}, u32[]{:S(2)}, u32[]{:S(2)}) async-start(bf16[26,8,64,128]{3,2,0,1:T(8,128)(2,1)} %copy.87), calls=%async_computation.1 | async-start | bytes 6815744 | tf_op jit(solution)/shard_map/all_to_all | solution.py:105
  113.6 186.5 %all-reduce.3.cloned.1.call-start = ((), (), s32[]{:S(2)}) async-start(), calls=%async_computation.2 | async-start | bytes 3932160 | tf_op jit(solution)/shard_map/psum | solution.py:101
  114.5 4.9 %copy-start.4 = (f32[729,351]{1,0:T(8,128)S(1)}, f32[729,351]{1,0:T(8,128)}, u32[]{:S(2)}) copy-start(f32[729,351]{1,0:T(8,128)} %constant.104.clone) | copy-start | bytes 3070552
  116.5 4.9 %copy-start.3 = (bf16[128,1024]{1,0:T(8,128)(2,1)S(1)}, bf16[128,1024]{1,0:T(8,128)(2,1)}, u32[]{:S(2)}) copy-start(bf16[128,1024]{1,0:T(8,128)(2,1)} %param.14) | copy-start | bytes 786436
  116.5 4.9 %copy-start.6 = (bf16[128,128]{0,1:T(8,128)(2,1)S(1)}, bf16[128,128]{0,1:T(8,128)(2,1)}, u32[]{:S(2)}) copy-start(bf16[128,128]{0,1:T(8,128)(2,1)} %copy.81) | copy-start | bytes 98308
  123.2 251.4 %all-reduce.5.cloned.1.call-start = ((), (), s32[]{:S(2)}) async-start(), calls=%async_computation.3 | async-start | bytes 6815744 | tf_op jit(solution)/shard_map/psum | solution.py:109
  374.6 3.2 copy-start.2
Sparse Core Ops, SparseCore 0:
  123.3 176.7 all-reduce.2
  303.0 71.5 all-reduce.4
where the time goes:
time: 389 us; the launch traced here: 386 us
  waiting for transfers between devices  160 us (41%)
  matrix products  105 us (27%)
  local copies, waits for them, and re-layouts  41.3 us (11%)
  blocking collectives  38 us (10%)
  other arithmetic  14.6 us (4%)
  between operations  14.3 us (4%)
  starting transfers between devices  12 us (3%)
    psum x1, waiting for transfers between devices, on_device(): table_grad = lax.psum(partial_value, 'rep')  74.5 us
    all_to_all x1, waiting for transfers between devices, on_device(): lax.all_to_all(grouped_rows, 'shard', split_axis=1, concat_axis=1, tiled=...  73.4 us
    dot_general x26, matrix products, per_table(): return jnp.dot(matches, table_rows, preferred_element_type=jnp.float32)  46.8 us
    dot_general x26, matrix products, place_table(): jnp.dot(placed.astype(jnp.bfloat16), table_rows, preferred_element_type=j...  45.3 us
    psum x1, blocking collectives, on_device(): top_grad, bias_grad = lax.psum((top_part, bias_part), ('rep', 'shard'))  38 us
    unnamed x25, local copies, waits for them, and re-layouts  11.4 us
    psum x1, waiting for transfers between devices, on_device(): top_grad, bias_grad = lax.psum((top_part, bias_part), ('rep', 'shard'))  10.4 us
  transfers between devices with their start and end apart: 4, of which 4 were waited for; matrix products, arithmetic and copies ran while one was open for 18% of the time, Pallas kernels for 0%

commit v1 on v0

--- a/solution.py
+++ b/solution.py
@@ -106,7 +106,8 @@
         lax.all_to_all(grouped_keys, "shard", split_axis=1, concat_axis=1, tiled=True),
         R_SHARD,
     )
-    table_grad = lax.psum(partial_value, "rep")
+    terms = lax.all_gather(partial_value, "rep")
+    table_grad = jnp.sum(terms, axis=0)
     return (dense_grad, top_grad, bias_grad, table_grad)
 
 

time: 389 us -> 467 us (1.20)
  waiting for transfers between devices: 160 us -> 230 us
  other arithmetic: 14.6 us -> 22.9 us
    psum x1, waiting for transfers between devices: 10.4 us -> 115 us  [on_device(): top_grad, bias_grad = lax.psum((top_part, bias_part), ('rep', 'shard'))]
    psum x1 -> x0, waiting for transfers between devices: 74.5 us -> none  [on_device(): table_grad = lax.psum(partial_value, 'rep')]
    all_gather x0 -> x1, waiting for transfers between devices: none -> 38.8 us  [on_device(): terms = lax.all_gather(partial_value, 'rep')]
    reduce_sum x0 -> x1, other arithmetic: none -> 8.29 us  [on_device(): table_grad = jnp.sum(terms, axis=0)]
    unnamed x25 -> x18, local copies, waits for them, and re-layouts: 11.4 us -> 8.33 us
  transfers between devices with their start and end apart: 4 -> 4, of which waited for: 4 -> 4; matrix products, arithmetic and copies ran while one was open for 18% -> 5% of each run, Pallas kernels for 0% -> 0%
where the time goes in v1:
time: 467 us; the launch traced here: 465 us
  waiting for transfers between devices  230 us (49%)
  matrix products  105 us (22%)
  local copies, waits for them, and re-layouts  39.9 us (9%)
  blocking collectives  39.1 us (8%)
  other arithmetic  22.9 us (5%)
  between operations  15.7 us (3%)
  starting transfers between devices  12 us (3%)
    psum x1, waiting for transfers between devices, on_device(): top_grad, bias_grad = lax.psum((top_part, bias_part), ('rep', 'shard'))  115 us
    all_to_all x1, waiting for transfers between devices, on_device(): lax.all_to_all(grouped_rows, 'shard', split_axis=1, concat_axis=1, tiled=...  73.6 us
    dot_general x26, matrix products, per_table(): return jnp.dot(matches, table_rows, preferred_element_type=jnp.float32)  46.8 us
    dot_general x26, matrix products, place_table(): jnp.dot(placed.astype(jnp.bfloat16), table_rows, preferred_element_type=j...  45.3 us
    psum x1, blocking collectives, on_device(): top_grad, bias_grad = lax.psum((top_part, bias_part), ('rep', 'shard'))  39.1 us
    all_gather x1, waiting for transfers between devices, on_device(): terms = lax.all_gather(partial_value, 'rep')  38.8 us
  transfers between devices with their start and end apart: 4, of which 4 were waited for; matrix products, arithmetic and copies ran while one was open for 5% of the time, Pallas kernels for 0%

profile of v1, /device:TPU:0, one launch (start us, length us, event | category | flops | bytes accessed | tf_op | source)
XLA Modules:
  0.0 464.9 jit_solution(4711469768007046253)
XLA Ops:
  11.3 2.0 fusion.17
  17.4 1.8 fusion.15
  19.2 2.9 copy.79
  22.1 2.4 copy.76
  24.5 1.8 fusion.16
  26.3 2.8 copy.78
  29.2 2.2 add.76
  35.2 2.3 broadcast_in_dim.67
  37.5 57.8 %while.25 = (s32[]{:T(128)}, bf16[26,512,128]{2,1,0:T(8,128)(2,1)}, s32[26,512]{1,0:T(8,128)S(1)}, s32[26,256]{1,0:T(8,128)S(1)}, bf16[26,256,128]{2,1,0:T(8,128)(2,1)}, /*index=5*/s32[]{:T(128)}, s32[]{:T(128)}) while((s32[]{:T(128)}, bf16[26,512,128]{2,1,0:T(8,128)(2,1)}, s32[26,512]{1,0:T(8,128)S(1)}, s32[26,256]{1,0:T(8,128)S(1)}, ...), condition=%wide.region_6.7_spmd, body=%wide.region_3.6_spmd.sunk | while | flops 34486784 | bytes 224349 | solution.py:100
  96.2 7.3 %all-to-all-start = ((s32[8,1,1664]{2,1,0:T(1,128)}), s32[8,1,1664]{2,1,0:T(1,128)S(1)}, u32[]{:S(2)}, u32[]{:S(2)}) async-start(s32[8,1,1664]{2,1,0:T(1,128)} %reshape.99), calls=%async_computation | async-start | bytes 106496 | tf_op jit(solution)/shard_map/all_to_all | solution.py:106
  103.5 4.8 %copy.87 = bf16[26,8,64,128]{3,2,0,1:T(8,128)(2,1)} copy(bf16[26,8,64,128]{3,2,1,0:T(8,128)(2,1)} %bitcast.73) | data formatting | bytes 6815744 | tf_op jit(solution)/shard_map/reshape | solution.py:102
  108.3 2.0 all-to-all-done
  110.3 4.5 all-to-all-start.1
  116.6 73.6 %all-to-all-done.1 = bf16[26,8,64,128]{3,2,0,1:T(8,128)(2,1)} async-done(((bf16[26,8,64,128]{3,2,0,1:T(8,128)(2,1)}), bf16[26,8,64,128]{3,2,0,1:T(8,128)(2,1)}, u32[]{:S(2)}, u32[]{:S(2)}) %all-to-all-start.1) | async-done | bytes 3407904 | tf_op jit(solution)/shard_map/all_to_all | solution.py:105
  190.2 4.8 %copy.88 = bf16[26,8,64,128]{3,2,1,0:T(8,128)(2,1)} copy(bf16[26,8,64,128]{3,2,0,1:T(8,128)(2,1)} %all-to-all-done.1) | data formatting | bytes 6815744 | tf_op jit(solution)/shard_map/all_to_all | solution.py:105
  195.0 47.0 %while.26 = (s32[]{:T(128)}, f32[26,256,128]{2,1,0:T(8,128)}, s32[26,512]{1,0:T(8,128)S(1)}, bf16[26,512,128]{2,1,0:T(8,128)(2,1)}, s32[]{:T(128)}) while((s32[]{:T(128)}, f32[26,256,128]{2,1,0:T(8,128)}, s32[26,512]{1,0:T(8,128)S(1)}, bf16[26,512,128]{2,1,0:T(8,128)(2,1)}, s32[]{:T(128)}) %tuple.72), condition=%wide.region_8.9_spmd, body=%wide.region_7.8_spmd.sunk | while | flops 33685504 | bytes 269385 | solution.py:22
  195.0 1.8 fusion.47
  196.8 1.8 fusion.47
  198.6 1.8 fusion.47
  200.4 1.8 fusion.47
  202.2 1.8 fusion.47
  204.0 1.8 fusion.47
  205.8 1.8 fusion.47
  207.6 1.8 fusion.47
  209.4 1.8 fusion.47
  211.2 1.8 fusion.47
  213.1 1.8 fusion.47
  214.9 1.8 fusion.47
  216.7 1.8 fusion.47
  218.5 1.8 fusion.47
  220.3 1.8 fusion.47
  222.1 1.8 fusion.47
  223.9 1.8 fusion.47
  225.7 1.8 fusion.47
  227.5 1.8 fusion.47
  229.3 1.8 fusion.47
  231.1 1.8 fusion.47
  232.9 1.8 fusion.47
  234.7 1.8 fusion.47
  238.3 1.8 fusion.47
  242.8 2.0 fusion.14
  244.8 2.9 reshape.98
  247.7 2.0 convolution_convert_fusion.1
  253.1 39.1 %psum.15 = f32[1024]{0:T(1024)} all-reduce(f32[1024]{0:T(1024)S(1)} %convert_reduce_fusion.1), channel_id=1, replica_groups=mesh['rep'=4,'shard'=8] {'rep','shard'}, use_global_device_ids=true, to_apply=%region_2.3 | all-reduce | flops 1024 | bytes 8192 | tf_op jit(solution)/shard_map/psum | solution.py:101
  292.2 38.8 %all-gather.3.cloned.1.call-done = f32[104,256,128]{2,1,0:T(8,128)} async-done(((f32[26,256,128]{2,1,0:T(8,128)}), f32[104,256,128]{2,1,0:T(8,128)}) %all-gather.3.cloned.1.call-update) | async-done | bytes 13631504 | tf_op jit(solution)/shard_map/all_gather | solution.py:109
  331.0 8.3 %reduce_sum.47 = f32[26,256,128]{2,1,0:T(8,128)} reduce(f32[4,26,256,128]{3,2,1,0:T(8,128)} %bitcast.72, f32[]{:T(128)} %constant.101.clone.1), dimensions={0}, to_apply=%region_9.10 | reduce | flops 2555904 | bytes 17039364 | tf_op jit(solution)/shard_map/reduce_sum | solution.py:110
  339.2 115.2 %all-reduce.2.cloned.1.call-done = f32[479,1024]{1,0:T(8,128)} async-done(((f32[479,1024]{1,0:T(8,128)}), f32[479,1024]{1,0:T(8,128)}) %all-reduce.2.cloned.1.call-update) | async-done | bytes 1962000 | tf_op jit(solution)/shard_map/psum | solution.py:101
  454.4 3.0 copy.114
  (304 shorter events, 78.6 us)
Async XLA Ops:
  8.0 2.0 copy-start
  8.0 3.3 copy-start.4
  31.4 1.2 copy-start.1
  96.2 14.1 %all-to-all-start = ((s32[8,1,1664]{2,1,0:T(1,128)}), s32[8,1,1664]{2,1,0:T(1,128)S(1)}, u32[]{:S(2)}, u32[]{:S(2)}) async-start(s32[8,1,1664]{2,1,0:T(1,128)} %reshape.99), calls=%async_computation | async-start | bytes 106496 | tf_op jit(solution)/shard_map/all_to_all | solution.py:106
  110.3 79.8 %all-to-all-start.1 = ((bf16[26,8,64,128]{3,2,0,1:T(8,128)(2,1)}), bf16[26,8,64,128]{3,2,0,1:T(8,128)(2,1)}, u32[]{:S(2)}, u32[]{:S(2)}) async-start(bf16[26,8,64,128]{3,2,0,1:T(8,128)(2,1)} %copy.87), calls=%async_computation.1 | async-start | bytes 6815744 | tf_op jit(solution)/shard_map/all_to_all | solution.py:105
  114.8 216.2 %all-gather.3.cloned.1.call-start = ((), (), s32[]{:S(2)}) async-start(), calls=%async_computation.3 | async-start | bytes 17039360 | tf_op jit(solution)/shard_map/all_gather | solution.py:109
  241.9 0.8 copy-start.5
  242.0 212.4 %all-reduce.2.cloned.1.call-start = ((), (), s32[]{:S(2)}) async-start(), calls=%async_computation.2 | async-start | bytes 3932160 | tf_op jit(solution)/shard_map/psum | solution.py:101
  242.8 4.8 %copy-start.3 = (f32[729,351]{1,0:T(8,128)S(1)}, f32[729,351]{1,0:T(8,128)}, u32[]{:S(2)}) copy-start(f32[729,351]{1,0:T(8,128)} %constant.104.clone) | copy-start | bytes 3070552
  244.8 4.9 %copy-start.2 = (bf16[128,1024]{1,0:T(8,128)(2,1)S(1)}, bf16[128,1024]{1,0:T(8,128)(2,1)}, u32[]{:S(2)}) copy-start(bf16[128,1024]{1,0:T(8,128)(2,1)} %param.14) | copy-start | bytes 786436
Sparse Core Ops, SparseCore 0:
  242.1 88.8 all-gather.2
Sparse Core Ops, SparseCore 1:
  251.5 202.9 all-reduce.1
